TPU v7x, 32 devices: a whole 2x2x4 slice. The times are simulated.
32 devices in a mesh: fluid: 8 (over y, x, core), solid: 4 (over z).
Axes of the slice: x: 2, y: 2, z: 4, core: 2. Of those that a mesh axis runs over, the one named last changes fastest.
Arguments:
- rbf_blocks: bfloat16 [3328, 256, 256], P(('fluid', 'solid')), may hold values from -0.375 to 0.375
- fluid_traction: bfloat16 [3328, 768], P(('fluid', 'solid')), may hold values from -24 to 24
- fluid_mass: bfloat16 [3328, 768], P(('fluid', 'solid')), may hold values from 0.19921875 to 2
- route: int32 [3328, 1], P(('fluid', 'solid')), may hold values from 0 to 31; in each aligned block of 104 rows (0 to 103, 104 to 207, ...) at most 6 rows name the same one
- slot: int32 [3328], P(('fluid', 'solid')), may hold values from 0 to 7
- shell_inverse: bfloat16 [256, 768, 768], P(('fluid', 'solid')), may hold values from -0.0078125 to 0.0078125
- robin_coef: float32 [256, 768], P(('fluid', 'solid')), may hold values from 1 to 27
- shell_start: float32 [256, 768], P(('fluid', 'solid')), may hold values from -3 to 3
Outputs:
- shell_displacement: float32 [256, 768], P(('fluid', 'solid'))
- fluid_load: bfloat16 [3328, 768], P(('fluid', 'solid'))
- residual_norms: float32 [6], replicated
Inputs may be any that keep to these rules, and one draw needn't show every extreme that they name: `route`: among the 104 blocks of one device at most 6 name the same owner device.
All inputs are finite; a program needn't handle non-finite values.
Results may differ from a plain program's by a relative error of at most 0.009.
Values may be sent and summed in bfloat16 or wider, within the bound.
A program may use at most 128 MiB of HBM per device.

v0:
```python
import jax
import jax.numpy as jnp
from jax import lax
from jax.sharding import PartitionSpec as P

ITERS = 6


RELAX = 0.3
EPSILON = 1e-06


def transport(buffer, devices, capacity):
    breadth = buffer.shape[1]
    moved = lax.all_to_all(
        buffer.reshape(devices, capacity, breadth),
        ("fluid", "solid"),
        split_axis=0,
        concat_axis=0,
        tiled=True,
    )
    return moved.reshape(devices * capacity, breadth)


def least_squares(gram, target_side):
    order = gram.shape[0]
    lower = [[None] * order for _ in range(order)]
    for row in range(order):
        for column in range(row + 1):
            total = gram[row, column]
            for inner in range(column):
                total = total - lower[row][inner] * lower[column][inner]
            if row == column:
                lower[row][row] = jnp.sqrt(total)
            else:
                lower[row][column] = total / lower[column][column]
    middle = []
    for row in range(order):
        total = target_side[row]
        for inner in range(row):
            total = total - lower[row][inner] * middle[inner]
        middle.append(total / lower[row][row])
    result = [None] * order
    for row in reversed(range(order)):
        total = middle[row]
        for inner in range(row + 1, order):
            total = total - lower[inner][row] * result[inner]
        result[row] = total / lower[row][row]
    return jnp.stack(result)


def per_device(
    rbf_blocks, fluid_traction, fluid_mass, route, slot, shell_inverse, robin_coef, shell_start
):
    devices = lax.axis_size("fluid") * lax.axis_size("solid")
    blocks = rbf_blocks.shape[0]
    nodes = rbf_blocks.shape[1]
    breadth = 3 * nodes
    shells = shell_inverse.shape[0]
    capacity = max(2, 2 * blocks // devices)
    slots_all = devices * capacity
    destination = route[:, 0]
    block_order = jnp.arange(blocks, dtype=jnp.int32)
    earlier = (destination[:, None] == destination[None, :]) & (
        block_order[None, :] < block_order[:, None]
    )
    slot_rank = jnp.sum(earlier.astype(jnp.int32), axis=1)
    position = destination * capacity + slot_rank
    positions = jnp.arange(slots_all, dtype=jnp.int32)
    placing = positions[:, None] == position[None, :]
    place_out = placing.astype(jnp.bfloat16)
    place_in = (position[:, None] == positions[None, :]).astype(jnp.bfloat16)
    wanted = jnp.max(jnp.where(placing, slot[None, :] + 1, 0), axis=1) - 1
    asked = lax.all_to_all(
        wanted.reshape(devices, capacity),
        ("fluid", "solid"),
        split_axis=0,
        concat_axis=0,
        tiled=True,
    ).reshape(slots_all)
    shell_ids = jnp.arange(shells, dtype=jnp.int32)
    picking = (asked[:, None] == shell_ids[None, :]).astype(jnp.bfloat16)
    collecting = (shell_ids[:, None] == asked[None, :]).astype(jnp.bfloat16)
    traction = fluid_traction.astype(jnp.float32)
    massive = fluid_mass.astype(jnp.float32)
    count = shells * devices * breadth
    current = shell_start
    residuals = []
    images = []
    norms = []
    last_load = None
    for iteration in range(ITERS):
        current_half = current.astype(jnp.bfloat16)
        outgoing = jnp.dot(picking, current_half, preferred_element_type=jnp.float32).astype(
            jnp.bfloat16
        )
        incoming = transport(outgoing, devices, capacity)
        displaced = jnp.dot(place_in, incoming, preferred_element_type=jnp.float32).astype(
            jnp.bfloat16
        )
        moved = jnp.einsum(
            "bcj,bij->bci",
            displaced.reshape(blocks, 3, nodes),
            rbf_blocks,
            preferred_element_type=jnp.float32,
        ).reshape(blocks, breadth)
        load = (traction - massive * moved).astype(jnp.bfloat16)
        last_load = load
        mapped = (
            jnp.einsum(
                "bci,bij->bcj",
                load.reshape(blocks, 3, nodes),
                rbf_blocks,
                preferred_element_type=jnp.float32,
            )
            .reshape(blocks, breadth)
            .astype(jnp.bfloat16)
        )
        sending = jnp.dot(place_out, mapped, preferred_element_type=jnp.float32).astype(
            jnp.bfloat16
        )
        arrived = transport(sending, devices, capacity)
        shell_load = jnp.dot(collecting, arrived, preferred_element_type=jnp.float32)
        forcing = (shell_load + robin_coef * current).astype(jnp.bfloat16)
        image = jnp.einsum("bi,bij->bj", forcing, shell_inverse, preferred_element_type=jnp.float32)
        residual = image - current
        residuals.append(residual)
        images.append(image)
        squares_local = jnp.sum(residual * residual)
        if iteration == 0:
            gram_local = jnp.zeros((1, 1), jnp.float32)
            rhs_local = jnp.zeros((1,), jnp.float32)
        else:
            changes = jnp.stack(
                [(residuals[i + 1] - residuals[i]).reshape(-1) for i in range(iteration)]
            )
            gram_local = jnp.dot(changes, changes.T, precision=lax.Precision.HIGHEST)
            rhs_local = jnp.dot(changes, residual.reshape(-1), precision=lax.Precision.HIGHEST)
        gram, rhs, squares = lax.psum((gram_local, rhs_local, squares_local), ("fluid", "solid"))
        norms.append(jnp.sqrt(squares / count + EPSILON))
        if iteration == 0:
            current = current + RELAX * residual
        else:
            image_changes = jnp.stack([images[i + 1] - images[i] for i in range(iteration)])
            coefs = least_squares(gram, -rhs)
            current = image + jnp.tensordot(
                coefs, image_changes, axes=1, precision=lax.Precision.HIGHEST
            )
    return (current, last_load, jnp.stack(norms))


def solution(mesh):
    in_specs = (
        P(("fluid", "solid"), None, None),
        P(("fluid", "solid"), None),
        P(("fluid", "solid"), None),
        P(("fluid", "solid"), None),
        P(("fluid", "solid")),
        P(("fluid", "solid"), None, None),
        P(("fluid", "solid"), None),
        P(("fluid", "solid"), None),
    )
    out_specs = (P(("fluid", "solid"), None), P(("fluid", "solid"), None), P())
    return jax.shard_map(
        per_device, mesh=mesh, in_specs=in_specs, out_specs=out_specs, check_vma=False
    )
```

profile of v0, /device:TPU:0, one launch (start us, length us, event | category | flops | bytes accessed | tf_op | source)
XLA Modules:
  0.0 597.5 jit_solution(4763548595876262729)
XLA Ops:
  0.6 0.9 convert_reduce_fusion
  2.5 14.3 %all_to_all.66 = s32[32,1,6]{2,1,0:T(1,128)S(1)} all-to-all(s32[32,1,6]{2,1,0:T(1,128)S(1)} %bitcast.395), channel_id=1, replica_groups=mesh['fluid'=8,'solid'=4] {'fluid','solid'}, dimensions={0} | all-to-all | bytes 1536 | tf_op jit(solution)/shard_map/all_to_all | solution.py:74
  18.1 1.0 convolution_convert_fusion.5
  19.1 0.8 reshape.209
  20.0 2.6 all-to-all-start.1
  22.6 1.1 copy.79
  23.7 1.1 copy.80
  25.4 9.0 %all-to-all-done.1 = bf16[32,6,768]{2,1,0:T(8,128)(2,1)S(1)} async-done(((bf16[32,6,768]{2,1,0:T(8,128)(2,1)}), bf16[32,6,768]{2,1,0:T(8,128)(2,1)S(1)}, u32[]{:S(2)}, u32[]{:S(2)}) %all-to-all-start.1) | async-done | bytes 294944 | tf_op jit(solution)/shard_map/all_to_all | solution.py:15
  35.1 8.5 %fusion.112 = f32[104,3,256]{2,1,0:T(4,128)S(1)} fusion(bf16[104,3,256]{2,1,0:T(4,128)(2,1)S(1)} %copy.82, bf16[104,256,256]{2,1,0:T(8,128)(2,1)} %param.8), kind=kOutput, calls=%fused_computation.209 | convolution fusion | flops 40894464 | bytes 14110720 | tf_op jit(solution)/shard_map/bcj,bij->bci/dot_general | solution.py:101
  44.1 6.7 %convolution_convert_fusion.17 = bf16[104,3,256]{2,1,0:T(4,128)(2,1)S(1)} fusion(bf16[104,3,256]{2,1,0:T(4,128)(2,1)S(1)} %copy.84, bf16[104,256,256]{2,1,0:T(8,128)(2,1)} %param.8), kind=kOutput, calls=%fused_computation.17 | convolution fusion | flops 40974336 | bytes 13950976 | tf_op jit(solution)/shard_map/bci,bij->bcj/dot_general | solution.py:110
  51.4 15.4 %all_to_all.67 = bf16[32,6,768]{2,1,0:T(8,128)(2,1)S(1)} all-to-all(bf16[32,6,768]{2,1,0:T(8,128)(2,1)S(1)} %reshape.214), channel_id=1, replica_groups=mesh['fluid'=8,'solid'=4] {'fluid','solid'}, dimensions={0} | all-to-all | bytes 589824 | tf_op jit(solution)/shard_map/all_to_all | solution.py:15
  67.1 5.0 fusion.59
  72.5 15.9 %all_to_all.68 = bf16[32,6,768]{2,1,0:T(8,128)(2,1)S(1)} all-to-all(bf16[32,6,768]{2,1,0:T(8,128)(2,1)S(1)} %reshape.216), channel_id=1, replica_groups=mesh['fluid'=8,'solid'=4] {'fluid','solid'}, dimensions={0} | all-to-all | bytes 589824 | tf_op jit(solution)/shard_map/all_to_all | solution.py:15
  89.2 8.5 %fusion.113 = f32[104,3,256]{2,1,0:T(4,128)S(1)} fusion(bf16[104,3,256]{2,1,0:T(4,128)(2,1)S(1)} %copy.87, bf16[104,256,256]{2,1,0:T(8,128)(2,1)} %param.8), kind=kOutput, calls=%fused_computation.210 | convolution fusion | flops 40894464 | bytes 14110720 | tf_op jit(solution)/shard_map/bcj,bij->bci/dot_general | solution.py:101
  98.1 6.7 %convolution_convert_fusion.16 = bf16[104,3,256]{2,1,0:T(4,128)(2,1)S(1)} fusion(bf16[104,3,256]{2,1,0:T(4,128)(2,1)S(1)} %copy.89, bf16[104,256,256]{2,1,0:T(8,128)(2,1)} %param.8), kind=kOutput, calls=%fused_computation.16 | convolution fusion | flops 40974336 | bytes 13950976 | tf_op jit(solution)/shard_map/bci,bij->bcj/dot_general | solution.py:110
  105.4 15.5 %all_to_all.69 = bf16[32,6,768]{2,1,0:T(8,128)(2,1)S(1)} all-to-all(bf16[32,6,768]{2,1,0:T(8,128)(2,1)S(1)} %reshape.221), channel_id=1, replica_groups=mesh['fluid'=8,'solid'=4] {'fluid','solid'}, dimensions={0} | all-to-all | bytes 589824 | tf_op jit(solution)/shard_map/all_to_all | solution.py:15
  121.2 5.0 fusion.57
  126.9 40.0 %all-reduce.4 = (f32[1]{0:T(128)}, f32[1,1]{1,0:T(1,128)}) all-reduce(f32[1]{0:T(128)} %bitcast.16, f32[1,1]{1,0:T(1,128)} %bitcast.18), channel_id=1, replica_groups=mesh['fluid'=8,'solid'=4] {'fluid','solid'}, use_global_device_ids=true, to_apply=%region_2.3 | all-reduce | flops 2 | bytes 16 | tf_op jit(solution)/shard_map/psum | solution.py:139
  168.7 15.8 %all_to_all.70 = bf16[32,6,768]{2,1,0:T(8,128)(2,1)S(1)} all-to-all(bf16[32,6,768]{2,1,0:T(8,128)(2,1)S(1)} %reshape.224), channel_id=1, replica_groups=mesh['fluid'=8,'solid'=4] {'fluid','solid'}, dimensions={0} | all-to-all | bytes 589824 | tf_op jit(solution)/shard_map/all_to_all | solution.py:15
  185.2 8.5 %fusion.114 = f32[104,3,256]{2,1,0:T(4,128)S(1)} fusion(bf16[104,3,256]{2,1,0:T(4,128)(2,1)S(1)} %copy.92, bf16[104,256,256]{2,1,0:T(8,128)(2,1)} %param.8), kind=kOutput, calls=%fused_computation.211 | convolution fusion | flops 40894464 | bytes 14110720 | tf_op jit(solution)/shard_map/bcj,bij->bci/dot_general | solution.py:101
  194.1 6.7 %convolution_convert_fusion.15 = bf16[104,3,256]{2,1,0:T(4,128)(2,1)S(1)} fusion(bf16[104,3,256]{2,1,0:T(4,128)(2,1)S(1)} %copy.94, bf16[104,256,256]{2,1,0:T(8,128)(2,1)} %param.8), kind=kOutput, calls=%fused_computation.15 | convolution fusion | flops 40974336 | bytes 13950976 | tf_op jit(solution)/shard_map/bci,bij->bcj/dot_general | solution.py:110
  201.4 0.8 reshape.229
  202.2 4.0 all-to-all-start.6
  206.2 11.8 %all-to-all-done.6 = bf16[32,6,768]{2,1,0:T(8,128)(2,1)S(1)} async-done(((bf16[32,6,768]{2,1,0:T(8,128)(2,1)}), bf16[32,6,768]{2,1,0:T(8,128)(2,1)S(1)}, u32[]{:S(2)}, u32[]{:S(2)}) %all-to-all-start.6) | async-done | bytes 294944 | tf_op jit(solution)/shard_map/all_to_all | solution.py:15
  218.3 5.0 fusion.55
  225.1 39.8 %all-reduce.3 = (f32[2]{0:T(128)S(1)}, f32[2,2]{1,0:T(2,128)S(1)}) all-reduce(f32[2]{0:T(128)S(1)} %convolution_bitcast_fusion.3, f32[2,2]{1,0:T(2,128)S(1)} %fusion.63), channel_id=1, replica_groups=mesh['fluid'=8,'solid'=4] {'fluid','solid'}, use_global_device_ids=true, to_apply=%region_4.5 | all-reduce | flops 6 | bytes 48 | tf_op jit(solution)/shard_map/psum | solution.py:139
  270.3 15.6 %all_to_all.71 = bf16[32,6,768]{2,1,0:T(8,128)(2,1)S(1)} all-to-all(bf16[32,6,768]{2,1,0:T(8,128)(2,1)S(1)} %reshape.232), channel_id=1, replica_groups=mesh['fluid'=8,'solid'=4] {'fluid','solid'}, dimensions={0} | all-to-all | bytes 589824 | tf_op jit(solution)/shard_map/all_to_all | solution.py:15
  286.6 8.5 %fusion.115 = f32[104,3,256]{2,1,0:T(4,128)S(1)} fusion(bf16[104,3,256]{2,1,0:T(4,128)(2,1)S(1)} %copy.97, bf16[104,256,256]{2,1,0:T(8,128)(2,1)} %param.8), kind=kOutput, calls=%fused_computation.212 | convolution fusion | flops 40894464 | bytes 14110720 | tf_op jit(solution)/shard_map/bcj,bij->bci/dot_general | solution.py:101
  295.6 6.7 %convolution_convert_fusion.14 = bf16[104,3,256]{2,1,0:T(4,128)(2,1)S(1)} fusion(bf16[104,3,256]{2,1,0:T(4,128)(2,1)S(1)} %copy.99, bf16[104,256,256]{2,1,0:T(8,128)(2,1)} %param.8), kind=kOutput, calls=%fused_computation.14 | convolution fusion | flops 40974336 | bytes 13950976 | tf_op jit(solution)/shard_map/bci,bij->bcj/dot_general | solution.py:110
  302.9 15.5 %all_to_all.72 = bf16[32,6,768]{2,1,0:T(8,128)(2,1)S(1)} all-to-all(bf16[32,6,768]{2,1,0:T(8,128)(2,1)S(1)} %reshape.237), channel_id=1, replica_groups=mesh['fluid'=8,'solid'=4] {'fluid','solid'}, dimensions={0} | all-to-all | bytes 589824 | tf_op jit(solution)/shard_map/all_to_all | solution.py:15
  318.6 5.0 fusion.53
  325.4 39.8 %all-reduce.2 = (f32[3]{0:T(128)S(1)}, f32[3,3]{1,0:T(4,128)S(1)}) all-reduce(f32[3]{0:T(128)S(1)} %convolution_bitcast_fusion.2, f32[3,3]{1,0:T(4,128)S(1)} %fusion.31), channel_id=1, replica_groups=mesh['fluid'=8,'solid'=4] {'fluid','solid'}, use_global_device_ids=true, to_apply=%region_6.7 | all-reduce | flops 12 | bytes 96 | tf_op jit(solution)/shard_map/psum | solution.py:139
  373.3 15.8 %all_to_all.73 = bf16[32,6,768]{2,1,0:T(8,128)(2,1)S(1)} all-to-all(bf16[32,6,768]{2,1,0:T(8,128)(2,1)S(1)} %reshape.240), channel_id=1, replica_groups=mesh['fluid'=8,'solid'=4] {'fluid','solid'}, dimensions={0} | all-to-all | bytes 589824 | tf_op jit(solution)/shard_map/all_to_all | solution.py:15
  389.8 8.5 %fusion.116 = f32[104,3,256]{2,1,0:T(4,128)S(1)} fusion(bf16[104,3,256]{2,1,0:T(4,128)(2,1)S(1)} %copy.102, bf16[104,256,256]{2,1,0:T(8,128)(2,1)} %param.8), kind=kOutput, calls=%fused_computation.213 | convolution fusion | flops 40894464 | bytes 14110720 | tf_op jit(solution)/shard_map/bcj,bij->bci/dot_general | solution.py:101
  398.8 6.7 %convolution_convert_fusion.13 = bf16[104,3,256]{2,1,0:T(4,128)(2,1)S(1)} fusion(bf16[104,3,256]{2,1,0:T(4,128)(2,1)S(1)} %copy.104, bf16[104,256,256]{2,1,0:T(8,128)(2,1)} %param.8), kind=kOutput, calls=%fused_computation.13 | convolution fusion | flops 40974336 | bytes 13950976 | tf_op jit(solution)/shard_map/bci,bij->bcj/dot_general | solution.py:110
  406.1 15.5 %all_to_all.74 = bf16[32,6,768]{2,1,0:T(8,128)(2,1)S(1)} all-to-all(bf16[32,6,768]{2,1,0:T(8,128)(2,1)S(1)} %reshape.245), channel_id=1, replica_groups=mesh['fluid'=8,'solid'=4] {'fluid','solid'}, dimensions={0} | all-to-all | bytes 589824 | tf_op jit(solution)/shard_map/all_to_all | solution.py:15
  421.8 5.0 fusion.51
  426.8 0.7 multiply_reduce_fusion.3
  428.7 39.8 %all-reduce.1 = (f32[4]{0:T(128)S(1)}, f32[4,4]{1,0:T(4,128)S(1)}) all-reduce(f32[4]{0:T(128)S(1)} %convolution_bitcast_fusion.1, f32[4,4]{1,0:T(4,128)S(1)} %fusion.62), channel_id=1, replica_groups=mesh['fluid'=8,'solid'=4] {'fluid','solid'}, use_global_device_ids=true, to_apply=%region_8.9 | all-reduce | flops 20 | bytes 160 | tf_op jit(solution)/shard_map/psum | solution.py:139
  480.0 15.8 %all_to_all.75 = bf16[32,6,768]{2,1,0:T(8,128)(2,1)S(1)} all-to-all(bf16[32,6,768]{2,1,0:T(8,128)(2,1)S(1)} %reshape.248), channel_id=1, replica_groups=mesh['fluid'=8,'solid'=4] {'fluid','solid'}, dimensions={0} | all-to-all | bytes 589824 | tf_op jit(solution)/shard_map/all_to_all | solution.py:15
  496.6 8.5 %fusion.117 = f32[104,3,256]{2,1,0:T(4,128)S(1)} fusion(bf16[104,3,256]{2,1,0:T(4,128)(2,1)S(1)} %copy.107, bf16[104,256,256]{2,1,0:T(8,128)(2,1)} %param.8), kind=kOutput, calls=%fused_computation.214 | convolution fusion | flops 40894464 | bytes 14110720 | tf_op jit(solution)/shard_map/bcj,bij->bci/dot_general | solution.py:101
  505.5 6.7 %convolution_convert_fusion.12 = bf16[104,3,256]{2,1,0:T(4,128)(2,1)S(1)} fusion(bf16[104,3,256]{2,1,0:T(4,128)(2,1)S(1)} %copy.109, bf16[104,256,256]{2,1,0:T(8,128)(2,1)} %param.8), kind=kOutput, calls=%fused_computation.12 | convolution fusion | flops 40974336 | bytes 13950976 | tf_op jit(solution)/shard_map/bci,bij->bcj/dot_general | solution.py:110
  512.7 0.8 reshape.253
  513.6 3.8 all-to-all-start.12
  517.4 0.8 copy.111
  518.2 11.0 %all-to-all-done.12 = bf16[32,6,768]{2,1,0:T(8,128)(2,1)S(1)} async-done(((bf16[32,6,768]{2,1,0:T(8,128)(2,1)}), bf16[32,6,768]{2,1,0:T(8,128)(2,1)S(1)}, u32[]{:S(2)}, u32[]{:S(2)}) %all-to-all-start.12) | async-done | bytes 294944 | tf_op jit(solution)/shard_map/all_to_all | solution.py:15
  529.5 5.0 fusion.49
  536.5 40.1 %all-reduce = (f32[5]{0:T(128)S(1)}, f32[5,5]{1,0:T(8,128)S(1)}, f32[]{:T(128)}, f32[]{:T(128)}, f32[]{:T(128)}, /*index=5*/f32[]{:T(128)}, f32[]{:T(128)}, f32[]{:T(128)}) all-reduce(f32[5]{0:T(128)S(1)} %convolution_bitcast_fusion, f32[5,5]{1,0:T(8,128)S(1)} %fusion.118, ...), channel_id=1, replica_groups=mesh['fluid'=8,'solid'=4] {'fluid','solid'}, use_global_device_ids=true, to_apply=%region_10.11 | all-reduce | flops 36 | bytes 288 | tf_op jit(solution)/shard_map/psum | solution.py:139
  (148 shorter events, 31.8 us)
Async XLA Ops:
  20.0 14.4 %all-to-all-start.1 = ((bf16[32,6,768]{2,1,0:T(8,128)(2,1)}), bf16[32,6,768]{2,1,0:T(8,128)(2,1)S(1)}, u32[]{:S(2)}, u32[]{:S(2)}) async-start(bf16[32,6,768]{2,1,0:T(8,128)(2,1)} %reshape.209), calls=%async_computation.1 | async-start | bytes 786432 | tf_op jit(solution)/shard_map/all_to_all | solution.py:15
  43.8 23.1 %copy-start = (f32[8,768]{1,0:T(8,128)S(1)}, f32[8,768]{1,0:T(8,128)}, u32[]{:S(2)}) copy-start(f32[8,768]{1,0:T(8,128)} %param.14) | copy-start | bytes 73732
  43.8 23.1 %copy-start.1 = (f32[8,768]{1,0:T(8,128)S(1)}, f32[8,768]{1,0:T(8,128)}, u32[]{:S(2)}) copy-start(f32[8,768]{1,0:T(8,128)} %param.15) | copy-start | bytes 73732
  202.2 15.8 %all-to-all-start.6 = ((bf16[32,6,768]{2,1,0:T(8,128)(2,1)}), bf16[32,6,768]{2,1,0:T(8,128)(2,1)S(1)}, u32[]{:S(2)}, u32[]{:S(2)}) async-start(bf16[32,6,768]{2,1,0:T(8,128)(2,1)} %reshape.229), calls=%async_computation.6 | async-start | bytes 786432 | tf_op jit(solution)/shard_map/all_to_all | solution.py:15
  513.6 15.7 %all-to-all-start.12 = ((bf16[32,6,768]{2,1,0:T(8,128)(2,1)}), bf16[32,6,768]{2,1,0:T(8,128)(2,1)S(1)}, u32[]{:S(2)}, u32[]{:S(2)}) async-start(bf16[32,6,768]{2,1,0:T(8,128)(2,1)} %reshape.253), calls=%async_computation.12 | async-start | bytes 786432 | tf_op jit(solution)/shard_map/all_to_all | solution.py:15
where the time goes:
time: 605 us; the launch traced here: 598 us
  blocking collectives  355 us (59%)
  matrix products  133 us (22%)
  between operations  39.3 us (6%)
  waiting for transfers between devices  31.8 us (5%)
  local copies, waits for them, and re-layouts  20.5 us (3%)
  starting transfers between devices  10.4 us (2%)
  other arithmetic  7.47 us (1%)
    psum x5, blocking collectives, per_device(): lax.psum((gram_local, rhs_local, squares_local), ('fluid', 'solid'))  200 us
    all_to_all x9, blocking collectives, transport(): lax.all_to_all(buffer.reshape(devices, capacity, breadth), ('fluid', 'sol...  141 us
    dot_general x6, matrix products, per_device(): jnp.einsum('bcj,bij->bci', displaced.reshape(blocks, 3, nodes), rbf_block...  50.9 us
    dot_general x6, matrix products, per_device(): jnp.einsum('bci,bij->bcj', load.reshape(blocks, 3, nodes), rbf_blocks, pr...  40.5 us
    all_to_all x3, waiting for transfers between devices, transport(): lax.all_to_all(buffer.reshape(devices, capacity, breadth), ('fluid', 'sol...  31.8 us
    dot_general x6, matrix products, per_device(): jnp.einsum('bi,bij->bj', forcing, shell_inverse, preferred_element_type=j...  30.1 us
    all_to_all x1, blocking collectives, per_device(): lax.all_to_all(wanted.reshape(devices, capacity), ('fluid', 'solid'), spl...  14.3 us
  transfers between devices with their start and end apart: 3, of which 3 were waited for; matrix products, arithmetic and copies ran while one was open for 1% of the time, Pallas kernels for 0%

commit v1 on v0

--- a/solution.py
+++ b/solution.py
@@ -1,6 +1,10 @@
+import functools
+
 import jax
 import jax.numpy as jnp
 from jax import lax
+from jax.experimental import pallas as pl
+from jax.experimental.pallas import tpu as pltpu
 from jax.sharding import PartitionSpec as P
 
 ITERS = 6
@@ -149,6 +153,410 @@
     return (current, last_load, jnp.stack(norms))
 
 
+CHUNK = 8
+LANES = 128
+VMEM_BYTES = 67043328
+MESH = pl.DeviceIdType.MESH
+
+
+def kernel(
+    nf, nz, blocks, nodes, shells, count,
+    key_ref, row_ref, tr_ref, ms_ref, robin_ref, start_ref, rbf_hbm, inv_hbm,
+    cur_out, load_out, norm_out,
+    rbf, inv, slots, curb, cur_own, vhist, rprev, sc, place, collect, disp, loadf, mapped,
+    part, send_a, recv_a, send_b, recv_b, send_c, recv_c, shell_sum,
+    rbf_sem, inv_sem,
+    s1, r1, s2, r2, s3, r3, sa, ra, sb, rb, sc_s, sc_r,
+):
+    f32, bf16 = jnp.float32, jnp.bfloat16
+    breadth = 3 * nodes
+    nxy = nf // 2
+    group = nz * shells
+    every = nf * group
+    f = lax.axis_index("fluid")
+    z = lax.axis_index("solid")
+    xy = f // 2
+    core = lax.rem(f, 2)
+    other = 1 - core
+    nchunk = blocks // CHUNK
+    rows = disp.shape[0]
+
+    def turn(value, step, size):
+        return lax.rem(value + step + size, size)
+
+    def fluid_of(plane, unit):
+        return plane * 2 + unit
+
+    def first_row(plane, unit, depth):
+        return pl.multiple_of((fluid_of(plane, unit) * nz + depth) * shells, shells)
+
+    def rbf_copy(i):
+        at = pl.ds(i * CHUNK, CHUNK)
+        return pltpu.make_async_copy(rbf_hbm.at[at], rbf.at[at], rbf_sem.at[i])
+
+    def inv_copy():
+        return pltpu.make_async_copy(inv_hbm, inv, inv_sem)
+
+    def start_rbf(i, carry):
+        rbf_copy(i).start()
+        return carry
+
+    lax.fori_loop(0, nchunk, start_rbf, 0)
+    inv_copy().start()
+
+    own_row = first_row(xy, core, z)
+    for j in range(ITERS + 1):
+        slots[j] = jnp.zeros(slots.shape[1:], f32)
+    slots[0, pl.ds(own_row, shells), 0:breadth] = start_ref[...]
+    vhist[...] = jnp.zeros(vhist.shape, f32)
+    sc[...] = jnp.zeros(sc.shape, f32)
+    rprev[...] = jnp.zeros(rprev.shape, f32)
+    mapped[...] = jnp.zeros(mapped.shape, f32)
+    loadf[...] = jnp.zeros(loadf.shape, f32)
+
+    barrier = pltpu.get_barrier_semaphore()
+    for d in range(1, nz):
+        pl.semaphore_signal(barrier, inc=1, device_id=(f, turn(z, d, nz)), device_id_type=MESH)
+    for e in range(1, nxy):
+        pl.semaphore_signal(
+            barrier, inc=1, device_id=(fluid_of(turn(xy, e, nxy), core), z), device_id_type=MESH
+        )
+    pl.semaphore_signal(barrier, inc=1, device_id=(fluid_of(xy, other), z), device_id_type=MESH)
+
+    place[...] = jnp.where(
+        key_ref[...] == lax.broadcasted_iota(jnp.int32, (rows, 3 * every), 1), 1.0, 0.0
+    ).astype(bf16)
+    for side in range(2):
+        unit = core if side == 0 else other
+        line = lax.broadcasted_iota(jnp.int32, (nxy * group, 1), 0)
+        ids = (line // group * 2 + unit) * group + lax.rem(line, group)
+        for c in range(3):
+            collect[side, c] = jnp.where(ids + c * every == row_ref[...], 1.0, 0.0).astype(bf16)
+
+    pl.semaphore_wait(barrier, (nz - 1) + (nxy - 1) + 1)
+
+    def all_gather(j, lanes):
+        def block(plane, unit, depth):
+            return slots.at[j, pl.ds(first_row(plane, unit, depth), shells), lanes]
+
+        def send(ref, send_sem, recv_sem, fluid, solid):
+            return pltpu.make_async_remote_copy(
+                src_ref=ref, dst_ref=ref, send_sem=send_sem, recv_sem=recv_sem,
+                device_id=(fluid, solid), device_id_type=MESH,
+            )
+
+        def along(d, incoming=False):
+            depth = turn(z, -d, nz) if incoming else z
+            return send(block(xy, core, depth), s1.at[d - 1], r1.at[d - 1], f, turn(z, d, nz))
+
+        def across(d, e, incoming=False):
+            plane = turn(xy, -e, nxy) if incoming else xy
+            return send(
+                block(plane, core, turn(z, -d, nz)), s2.at[d, e - 1], r2.at[d, e - 1],
+                fluid_of(turn(xy, e, nxy), core), z,
+            )
+
+        def pair(d, e, incoming=False):
+            unit = other if incoming else core
+            return send(
+                block(turn(xy, -e, nxy), unit, turn(z, -d, nz)), s3.at[d, e], r3.at[d, e],
+                fluid_of(xy, other), z,
+            )
+
+        for d in range(1, nz):
+            along(d).start()
+        for d in range(nz):
+            if d > 0:
+                along(d, True).wait_recv()
+            for e in range(1, nxy):
+                across(d, e).start()
+            pair(d, 0).start()
+        for d in range(nz):
+            for e in range(1, nxy):
+                across(d, e, True).wait_recv()
+                pair(d, e).start()
+        for d in range(nz):
+            for e in range(nxy):
+                pair(d, e, True).wait_recv()
+        for d in range(1, nz):
+            along(d).wait_send()
+        for d in range(nz):
+            for e in range(1, nxy):
+                across(d, e).wait_send()
+            for e in range(nxy):
+                pair(d, e).wait_send()
+
+    lane = lax.broadcasted_iota(jnp.int32, (1, LANES), 1)
+
+    def pick(vector, q):
+        return jnp.sum(jnp.where(lane == q, vector, 0.0), axis=1, keepdims=True)
+
+    def coefficients(j):
+        k = j - 1
+        total = jnp.sum(slots[j, :, breadth:], axis=0, keepdims=True)
+        sc[j] = total
+        norm = jnp.sqrt(pick(total, 0) / count + EPSILON)
+
+        @pl.when(j > 0)
+        def _():
+            norm_out[jnp.maximum(k, 0)] = jnp.broadcast_to(norm, (1, LANES))
+
+        order = ITERS - 1
+        gram = [[None] * order for _ in range(order)]
+        for col in range(order):
+            vector = sc[col + 2]
+            for row in range(col + 1):
+                value = pick(vector, 8 + row)
+                if row == col:
+                    value = jnp.where(col < k, value, 1.0)
+                gram[col][row] = value
+        side = [-pick(total, 1 + i) for i in range(order)]
+        lower = [[None] * order for _ in range(order)]
+        for row in range(order):
+            for col in range(row + 1):
+                value = gram[row][col]
+                for inner in range(col):
+                    value = value - lower[row][inner] * lower[col][inner]
+                if row == col:
+                    lower[row][row] = jnp.sqrt(value)
+                else:
+                    lower[row][col] = value / lower[col][col]
+        middle = []
+        for row in range(order):
+            value = side[row]
+            for inner in range(row):
+                value = value - lower[row][inner] * middle[inner]
+            middle.append(value / lower[row][row])
+        result = [None] * order
+        for row in reversed(range(order)):
+            value = middle[row]
+            for inner in range(row + 1, order):
+                value = value - lower[inner][row] * result[inner]
+            result[row] = value / lower[row][row]
+        relax = jnp.where(j == 1, jnp.full((1, 1), RELAX - 1.0, f32), 0.0)
+        return [relax] + result
+
+    def combine(j, coefs, at):
+        value = slots[j, at, 0:breadth]
+        before = slots[0, at, 0:breadth]
+        for i in range(ITERS):
+            after = slots[i + 1, at, 0:breadth]
+            value = value + coefs[i] * (after - before)
+            before = after
+        return value
+
+    def dot(a, b, dims=((1,), (0,))):
+        return lax.dot_general(a, b, (dims, ((), ())), preferred_element_type=f32)
+
+    def iteration(j, carry):
+        all_gather(j, pl.ds(0, breadth + LANES))
+        coefs = coefficients(j)
+
+        def update(i, c):
+            at = pl.ds(pl.multiple_of(i * 16, 16), 16)
+            curb[at, :] = combine(j, coefs, at).astype(bf16)
+            return c
+
+        lax.fori_loop(0, every // 16, update, 0)
+        cur_own[...] = combine(j, coefs, pl.ds(own_row, shells))
+        picked = None
+        for c in range(3):
+            term = dot(
+                place[:, c * every:(c + 1) * every], curb[:, c * nodes:(c + 1) * nodes]
+            )
+            picked = term if picked is None else picked + term
+        disp[...] = picked
+
+        def fluid(i, c):
+            @pl.when(j == 0)
+            def _():
+                rbf_copy(i).wait()
+
+            loads = []
+            for u in range(CHUNK):
+                b = i * CHUNK + u
+                at = pl.ds(pl.multiple_of(b * 8, 8), 8)
+                moved = dot(disp[at, :].astype(bf16), rbf[b], ((1,), (1,)))
+                load = (tr_ref[at, :] - ms_ref[at, :] * moved).astype(bf16)
+                loadf[at, :] = load.astype(f32)
+                loads.append(load)
+            for u in range(CHUNK):
+                b = i * CHUNK + u
+                at = pl.ds(pl.multiple_of(b * 8, 8), 8)
+                mapped[at, :] = dot(loads[u], rbf[b]).astype(bf16).astype(f32)
+            return c
+
+        lax.fori_loop(0, nchunk, fluid, 0)
+
+        mapped_half = mapped[...].astype(bf16)
+        for c in range(3):
+            send_a[:, c * nodes:(c + 1) * nodes] = dot(collect[1, c], mapped_half).astype(bf16)
+        copy_a = pltpu.make_async_remote_copy(
+            src_ref=send_a, dst_ref=recv_a, send_sem=sa, recv_sem=ra,
+            device_id=(fluid_of(xy, other), z), device_id_type=MESH,
+        )
+        copy_a.start()
+        for c in range(3):
+            part[:, c * nodes:(c + 1) * nodes] = dot(collect[0, c], mapped_half)
+        copy_a.wait_recv()
+        part[...] = part[...] + recv_a[...].astype(f32)
+
+        def copy_b(e):
+            return pltpu.make_async_remote_copy(
+                src_ref=send_b.at[e - 1], dst_ref=recv_b.at[e - 1],
+                send_sem=sb.at[e - 1], recv_sem=rb.at[e - 1],
+                device_id=(fluid_of(turn(xy, e, nxy), core), z), device_id_type=MESH,
+            )
+
+        for e in range(1, nxy):
+            at = pl.ds(pl.multiple_of(turn(xy, e, nxy) * group, group), group)
+            send_b[e - 1] = part[at, :].astype(bf16)
+            copy_b(e).start()
+        line = part[pl.ds(pl.multiple_of(xy * group, group), group), :]
+        for e in range(1, nxy):
+            copy_b(e).wait_recv()
+            line = line + recv_b[e - 1].astype(f32)
+        shell_sum[...] = line
+
+        def copy_c(d):
+            return pltpu.make_async_remote_copy(
+                src_ref=send_c.at[d - 1], dst_ref=recv_c.at[d - 1],
+                send_sem=sc_s.at[d - 1], recv_sem=sc_r.at[d - 1],
+                device_id=(f, turn(z, d, nz)), device_id_type=MESH,
+            )
+
+        for d in range(1, nz):
+            at = pl.ds(pl.multiple_of(turn(z, d, nz) * shells, shells), shells)
+            send_c[d - 1] = shell_sum[at, :].astype(bf16)
+            copy_c(d).start()
+        shell_load = shell_sum[pl.ds(pl.multiple_of(z * shells, shells), shells), :]
+        for d in range(1, nz):
+            copy_c(d).wait_recv()
+            shell_load = shell_load + recv_c[d - 1].astype(f32)
+        copy_a.wait_send()
+        for e in range(1, nxy):
+            copy_b(e).wait_send()
+        for d in range(1, nz):
+            copy_c(d).wait_send()
+
+        @pl.when(j == 0)
+        def _():
+            inv_copy().wait()
+
+        current = cur_own[...]
+        forcing = (shell_load + robin_ref[...] * current).astype(bf16)
+        shell_row = lax.broadcasted_iota(jnp.int32, (shells, breadth), 0)
+
+        def solid(s, image):
+            return jnp.where(shell_row == s, dot(forcing, inv[s]), image)
+
+        image = lax.fori_loop(0, shells, solid, jnp.zeros((shells, breadth), f32))
+        residual = image - current
+        newest = residual - rprev[...]
+        rprev[...] = residual
+        vhist[lax.rem(j + ITERS - 1, ITERS)] = newest
+        lane_rows = lax.broadcasted_iota(jnp.int32, (shells, LANES), 1)
+
+        def put(vector, q, product):
+            return jnp.where(lane_rows == q, jnp.sum(product, axis=1, keepdims=True), vector)
+
+        scalars = put(jnp.zeros((shells, LANES), f32), 0, residual * residual)
+        for i in range(ITERS - 1):
+            scalars = put(scalars, 1 + i, vhist[i] * residual)
+            scalars = put(scalars, 8 + i, vhist[i] * newest)
+        own = pl.ds(own_row, shells)
+        slots[j + 1, own, 0:breadth] = image
+        slots[j + 1, own, breadth:] = scalars
+        return carry
+
+    lax.fori_loop(0, ITERS, iteration, 0)
+    all_gather(ITERS, pl.ds(breadth, LANES))
+    cur_out[...] = combine(ITERS, coefficients(ITERS), pl.ds(own_row, shells))
+    load_out[...] = loadf[0:blocks * 8, :].astype(bf16)
+
+
+def fused(nf, nz, rbf_blocks, fluid_traction, fluid_mass, route, slot, shell_inverse, robin_coef, shell_start):
+    f32, bf16 = jnp.float32, jnp.bfloat16
+    blocks, nodes, _ = rbf_blocks.shape
+    shells, breadth = shell_start.shape
+    nxy = nf // 2
+    group = nz * shells
+    every = nf * group
+    rows = -(-blocks * 8 // LANES) * LANES
+    target = route[:, 0] * shells + slot
+    part_of = jnp.arange(8, dtype=jnp.int32)[None, :]
+    key = jnp.where(part_of < 3, target[:, None] + part_of * every, -1).reshape(-1)
+    key = jnp.pad(key, (0, rows - blocks * 8), constant_values=-1)
+
+    def spread(x):
+        return jnp.pad(
+            x.reshape(blocks, 3, nodes).astype(f32), ((0, 0), (0, 5), (0, 0))
+        ).reshape(blocks * 8, nodes)
+
+    dma = pltpu.SemaphoreType.DMA
+    vmem = pl.BlockSpec(memory_space=pltpu.VMEM)
+    anywhere = pl.BlockSpec(memory_space=pl.ANY)
+    current, load, norms = pl.pallas_call(
+        functools.partial(kernel, nf, nz, blocks, nodes, shells, every * breadth),
+        out_shape=(
+            jax.ShapeDtypeStruct((shells, breadth), f32),
+            jax.ShapeDtypeStruct((blocks * 8, nodes), bf16),
+            jax.ShapeDtypeStruct((ITERS, 1, LANES), f32),
+        ),
+        in_specs=[vmem] * 6 + [anywhere] * 2,
+        out_specs=(vmem, vmem, vmem),
+        scratch_shapes=[
+            pltpu.VMEM(rbf_blocks.shape, bf16),
+            pltpu.VMEM(shell_inverse.shape, bf16),
+            pltpu.VMEM((ITERS + 1, every, breadth + LANES), f32),
+            pltpu.VMEM((every, breadth), bf16),
+            pltpu.VMEM((shells, breadth), f32),
+            pltpu.VMEM((ITERS, shells, breadth), f32),
+            pltpu.VMEM((shells, breadth), f32),
+            pltpu.VMEM((ITERS + 1, 1, LANES), f32),
+            pltpu.VMEM((rows, 3 * every), bf16),
+            pltpu.VMEM((2, 3, nxy * group, rows), bf16),
+            pltpu.VMEM((rows, nodes), f32),
+            pltpu.VMEM((rows, nodes), f32),
+            pltpu.VMEM((rows, nodes), f32),
+            pltpu.VMEM((nxy * group, breadth), f32),
+            pltpu.VMEM((nxy * group, breadth), bf16),
+            pltpu.VMEM((nxy * group, breadth), bf16),
+            pltpu.VMEM((nxy - 1, group, breadth), bf16),
+            pltpu.VMEM((nxy - 1, group, breadth), bf16),
+            pltpu.VMEM((nz - 1, shells, breadth), bf16),
+            pltpu.VMEM((nz - 1, shells, breadth), bf16),
+            pltpu.VMEM((group, breadth), f32),
+            dma((blocks // CHUNK,)),
+            dma,
+            dma((nz - 1,)), dma((nz - 1,)),
+            dma((nz, nxy - 1)), dma((nz, nxy - 1)),
+            dma((nz, nxy)), dma((nz, nxy)),
+            dma, dma,
+            dma((nxy - 1,)), dma((nxy - 1,)),
+            dma((nz - 1,)), dma((nz - 1,)),
+        ],
+        compiler_params=pltpu.CompilerParams(
+            collective_id=0, has_side_effects=True, vmem_limit_bytes=VMEM_BYTES
+        ),
+        name="coupling",
+    )(
+        key[:, None], key[None, :], spread(fluid_traction), spread(fluid_mass),
+        robin_coef, shell_start, rbf_blocks, shell_inverse,
+    )
+    load = load.reshape(blocks, 8, nodes)[:, :3].reshape(blocks, breadth)
+    return current, load, norms[:, 0, 0]
+
+
+def choose(nf, nz):
+    def body(rbf_blocks, *others):
+        if nf * nz > 32:
+            return per_device(rbf_blocks, *others)
+        return fused(nf, nz, rbf_blocks, *others)
+
+    return body
+
+
 def solution(mesh):
     in_specs = (
         P(("fluid", "solid"), None, None),
@@ -162,5 +570,5 @@
     )
     out_specs = (P(("fluid", "solid"), None), P(("fluid", "solid"), None), P())
     return jax.shard_map(
-        per_device, mesh=mesh, in_specs=in_specs, out_specs=out_specs, check_vma=False
+        choose(mesh.shape["fluid"], mesh.shape["solid"]), mesh=mesh, in_specs=in_specs, out_specs=out_specs, check_vma=False
     )

time: 605 us -> 210 us (0.35); the launches traced: 598 us -> 209 us
  blocking collectives: 355 us -> 0 us
  Pallas kernels: 0 us -> 198 us
  matrix products: 133 us -> 0 us
  between operations: 39.3 us -> 0.69 us
  waiting for transfers between devices: 31.8 us -> 0 us
  local copies, waits for them, and re-layouts: 20.5 us -> 8.87 us
  starting transfers between devices: 10.4 us -> 0 us
    psum x5 -> x0, blocking collectives: 200 us -> none  [per_device(): lax.psum((gram_local, rhs_local, squares_local), ('fluid', 'solid'))]
    pallas_call x0 -> x1, Pallas kernels: none -> 198 us  [fused(): pl.pallas_call(functools.partial(kernel, nf, nz, blocks, nodes, shells, e...]
    all_to_all x10 -> x0, blocking collectives: 155 us -> none  [the longest x9 141 us: transport(): lax.all_to_all(buffer.reshape(devices, capacity, breadth), ('fluid', 'sol...]
    dot_general x54 -> x0, matrix products: 133 us -> none  [the longest x6 50.9 us: per_device(): jnp.einsum('bcj,bij->bci', displaced.reshape(blocks, 3, nodes), rbf_block...]
    all_to_all x3 -> x0, waiting for transfers between devices: 31.8 us -> none  [transport(): lax.all_to_all(buffer.reshape(devices, capacity, breadth), ('fluid', 'sol...]
    all_to_all x3 -> x0, starting transfers between devices: 10.4 us -> none  [transport(): lax.all_to_all(buffer.reshape(devices, capacity, breadth), ('fluid', 'sol...]
    reshape x36 -> x0, local copies, waits for them, and re-layouts: 6.8 us -> none  [the longest x12 3.42 us: transport(): buffer.reshape(devices, capacity, breadth)]
  transfers between devices with their start and end apart: 3 -> 0, of which waited for: 3 -> 0; matrix products, arithmetic and copies ran while one was open for 1% -> 0% of each run, Pallas kernels for 0% -> 0%
where the time goes in v1:
time: 210 us; the launch traced here: 209 us
  Pallas kernels  198 us (94%)
  local copies, waits for them, and re-layouts  8.87 us (4%)
  other arithmetic  2.1 us (1%)
    pallas_call x1, Pallas kernels, fused(): pl.pallas_call(functools.partial(kernel, nf, nz, blocks, nodes, shells, e...  198 us
    unnamed x5, local copies, waits for them, and re-layouts  4.51 us

profile of v1, /device:TPU:0, one launch (start us, length us, event | category | flops | bytes accessed | tf_op | source)
XLA Modules:
  0.0 209.3 jit_solution(4853147255035263262)
XLA Ops:
  0.6 0.7 bitcast_add_fusion
  1.3 0.1 add_select_fusion
  1.4 0.1 select_n.9
  1.5 0.6 broadcast_in_dim.23.row_ref
  2.1 1.1 copy.18
  3.2 0.2 copy.19
  3.4 1.1 copy.20
  4.4 0.2 copy.21
  4.6 0.9 broadcast_in_dim.24.key_ref
  5.6 1.3 bitcast_convert_fusion
  6.9 197.6 %coupling.1 = (f32[8,768]{1,0:T(8,128)}, bf16[832,256]{1,0:T(8,128)(2,1)}, f32[6,1,128]{2,1,0:T(1,128)}) custom-call(s32[896,1]{1,0:T(8,128)} %broadcast_in_dim.24.key_ref, s32[1,896]{1,0:T(1,128)} %broadcast_in_dim.23.row_ref, f32[832,256]{1,0:T(8,128)} %get-tuple-element.16.tr_ref, f32[832,256]{1,0:T(8,128)} %get-tuple-element.15.ms_ref, ...), custom_call_target="tpu_custom_call" | custom-call | tf_op jit(solution)/shard_map/coupling/pallas_call | solution.py:499
  204.6 1.1 slice.8
  205.6 0.2 copy.25
  205.8 0.8 copy.24
  206.6 1.3 slice_reduce_fusion
  207.9 1.3 copy.27
  (3 shorter events, 0.0 us)
